TPU v7x, 32 devices: a whole 2x2x4 slice. The times are simulated.
32 devices in a mesh: dist: 4 (over y, core), pix: 8 (over z, x).
Axes of the slice: x: 2, y: 2, z: 4, core: 2. Of those that a mesh axis runs over, the one named last changes fastest.
Arguments:
- contrast: float32 [4, 2, 2048, 2048], P('dist', None, 'pix'), may hold values from -6 to 6
- defocus: float32 [4], P('dist'), may hold values from 40 to 400
- blurring: float32 [4], P('dist'), may hold values from 0.5 to 4
Outputs:
- phase: float32 [2, 2048, 2048], P(None, 'pix')
All inputs are finite; a program needn't handle non-finite values.
Results may differ from a plain program's by a relative error of at most 0.0003.
Values sent between devices are 32-bit elements; how exact they have to be, the bound alone decides.
A program may use at most 64 MiB of HBM per device.

v0:
```python
import math
import jax
import jax.numpy as jnp
from jax import lax
from jax.sharding import PartitionSpec as P

ABSORB_RATIO = 0.1
REGULARIZER = 0.05


def unit_phase(first_len, second_len, period):
    left_index = jnp.arange(first_len, dtype=jnp.int32)[:, None]
    right_index = jnp.arange(second_len, dtype=jnp.int32)[None, :]
    turn_count = left_index * right_index % period
    angles = 2.0 * math.pi / period * turn_count.astype(jnp.float32)
    return (jnp.cos(angles), -jnp.sin(angles))


def conjugate_flip(tables):
    return (tables[0], -tables[1])


def complex_product(pattern, real_part, imag_part, tables):
    cosine, sine_part = tables
    out_real = jnp.einsum(pattern, real_part, cosine, precision=lax.Precision.HIGHEST) - jnp.einsum(
        pattern, imag_part, sine_part, precision=lax.Precision.HIGHEST
    )
    out_imag = jnp.einsum(
        pattern, real_part, sine_part, precision=lax.Precision.HIGHEST
    ) + jnp.einsum(pattern, imag_part, cosine, precision=lax.Precision.HIGHEST)
    return (out_real, out_imag)


def apply_twist(real_part, imag_part, cosine, sine_part):
    return (real_part * cosine - imag_part * sine_part, real_part * sine_part + imag_part * cosine)


def signed_square(freq_index, period):
    shifted = freq_index - period * (2 * freq_index >= period).astype(jnp.int32)
    fraction = shifted.astype(jnp.float32) / period
    return fraction * fraction


def transfer(defocus_value, blur_rate, squared):
    return jnp.exp(-blur_rate * squared) * (
        jnp.sin(defocus_value * squared) + ABSORB_RATIO * jnp.cos(defocus_value * squared)
    )


def body(contrast, defocus, blurring):
    images = contrast[0]
    projections, rows_local, columns = images.shape
    pix_count = lax.axis_size("pix")
    col_block = columns // pix_count
    rows_total = rows_local * pix_count
    outer_table = unit_phase(col_block, col_block, col_block)
    pixel_lookup_table = unit_phase(pix_count, pix_count, pix_count)
    row_table = unit_phase(rows_local, rows_local, rows_local)
    col_twist = unit_phase(col_block, pix_count, columns)
    row_twist = unit_phase(rows_local, pix_count, rows_total)
    even_images = images[0::2]
    odd_images = images[1::2]
    shaped_real = even_images.reshape(projections // 2, rows_local, col_block, pix_count)
    shaped_imag = odd_images.reshape(projections // 2, rows_local, col_block, pix_count)
    section_real, section_imag = complex_product(
        "prbn,bc->pcrn", shaped_real, shaped_imag, outer_table
    )
    section_real, section_imag = apply_twist(
        section_real, section_imag, col_twist[0][:, None, :], col_twist[1][:, None, :]
    )
    spec_real, spec_imag = complex_product(
        "pcrn,nq->pcrq", section_real, section_imag, pixel_lookup_table
    )
    col_freq = col_block * lax.axis_index("pix") + jnp.arange(col_block, dtype=jnp.int32)
    row_freq = (
        pix_count * jnp.arange(rows_local, dtype=jnp.int32)[:, None]
        + jnp.arange(pix_count, dtype=jnp.int32)[None, :]
    )
    squared = (
        signed_square(row_freq, rows_total)[None, :, :]
        + signed_square(col_freq, columns)[:, None, None]
    )
    own_gain = transfer(defocus[0], blurring[0], squared)
    received_real = lax.all_to_all(spec_real, "pix", split_axis=3, concat_axis=3, tiled=True)
    received_imaginary = lax.all_to_all(spec_imag, "pix", split_axis=3, concat_axis=3, tiled=True)
    middle_real, middle_imaginary = complex_product(
        "uhqb,bn->uhqn", received_real, received_imaginary, pixel_lookup_table
    )
    middle_real, middle_imaginary = apply_twist(
        middle_real, middle_imaginary, row_twist[0], row_twist[1]
    )
    out_real, out_imag = complex_product("pcrk,rj->pcjk", middle_real, middle_imaginary, row_table)
    summands = (own_gain * out_real, own_gain * out_imag, (own_gain * own_gain)[None])
    totals = lax.psum((summands[0], summands[1], summands[2]), "dist")
    den_sum = totals[2][0]
    bottom = 2.0 * (den_sum + REGULARIZER)
    quot_real = totals[0] / bottom
    quot_imag = totals[1] / bottom
    backward_real, backward_imaginary = complex_product(
        "pcjk,rj->pcrk", quot_real, quot_imag, conjugate_flip(row_table)
    )
    backward_real, backward_imaginary = apply_twist(
        backward_real, backward_imaginary, row_twist[0], -row_twist[1]
    )
    backward_real, backward_imaginary = complex_product(
        "uotv,zv->uotz", backward_real, backward_imaginary, conjugate_flip(pixel_lookup_table)
    )
    backward_real = backward_real / rows_total
    backward_imaginary = backward_imaginary / rows_total
    twist_cos = col_twist[0]
    twist_sin = col_twist[1]
    received_real = lax.all_to_all(backward_real, "pix", split_axis=3, concat_axis=3, tiled=True)
    received_imaginary = lax.all_to_all(
        backward_imaginary, "pix", split_axis=3, concat_axis=3, tiled=True
    )
    middle_real, middle_imaginary = complex_product(
        "pcrq,nq->pcrn", received_real, received_imaginary, conjugate_flip(pixel_lookup_table)
    )
    cols_real, cols_imag = apply_twist(
        middle_real, middle_imaginary, twist_cos[:, None, :], -twist_sin[:, None, :]
    )
    phase_blocks = jnp.einsum(
        "pcrn,cb->prbn", cols_real, outer_table[0], precision=lax.Precision.HIGHEST
    ) + jnp.einsum("pcrn,cb->prbn", cols_imag, outer_table[1], precision=lax.Precision.HIGHEST)
    odd_blocks = jnp.einsum(
        "pcrn,cb->prbn", cols_imag, outer_table[0], precision=lax.Precision.HIGHEST
    ) - jnp.einsum("pcrn,cb->prbn", cols_real, outer_table[1], precision=lax.Precision.HIGHEST)
    paired_blocks = jnp.stack([phase_blocks, odd_blocks], axis=1)
    return (paired_blocks / columns).reshape(projections, rows_local, columns)


def solution(mesh):
    return jax.shard_map(
        body,
        mesh=mesh,
        in_specs=(P("dist", None, "pix", None), P("dist"), P("dist")),
        out_specs=P(None, "pix", None),
        check_vma=False,
    )
```

profile of v0, /device:TPU:0, one launch (start us, length us, event | category | flops | bytes accessed | tf_op | source)
XLA Modules:
  0.0 490.3 jit_solution(7486254267559087429)
XLA Ops:
  6.6 3.9 fusion.322
  14.3 4.2 fusion.102
  18.5 4.2 fusion.90
  27.8 5.4 %convolution_subtract_fusion = f32[256,256,8]{1,0,2:T(8,128)S(1)} fusion(f32[256,256,8]{1,0,2:T(8,128)} %fusion.102, f32[256,256,8]{1,0,2:T(8,128)S(1)} %copy.80), kind=kOutput, calls=%fused_computation.91 | convolution fusion | flops 1612120064 | bytes 6291456 | tf_op jit(solution)/shard_map/prbn,bc->pcrn/dot_general | solution.py:25
  33.2 5.2 %multiply_subtract_fusion.2 = (f32[256,256,8]{1,0,2:T(8,128)S(1)}, f32[256,256,8]{1,0,2:T(8,128)S(1)}) fusion(f32[256,256,8]{1,0,2:T(8,128)S(1)} %convolution_subtract_fusion, f32[256,8]{0,1:T(8,128)S(1)} %get-tuple-element.19, f32[256,8]{0,1:T(8,128)S(1)} %get-tuple-element.18, f32[256,256,8]{1,0,2:T(8,128)S(1)} %copy-done.4, f32[256,256,8]{1,0,2:T(8,128)} %copy-done), kind=kOutput, calls=%fused_computation.59 | convolution fusion | flops 1615200256 | bytes 10502144 | tf_op jit(solution)/shard_map/prbn,bc->pcrn/dot_general | solution.py:30
  41.6 3.6 add_bitcast_fusion.1
  47.1 7.3 %all-to-all-start.1 = ((f32[1,256,256,8]{2,1,0,3:T(8,128)}), f32[1,256,256,8]{2,1,0,3:T(8,128)}, u32[]{:S(2)}, u32[]{:S(2)}) async-start(f32[1,256,256,8]{2,1,0,3:T(8,128)} %copy.94), calls=%async_computation.1 | async-start | bytes 4194304 | tf_op jit(solution)/shard_map/all_to_all | solution.py:85
  54.4 4.7 fusion.52
  64.3 38.4 %all-to-all-done.1 = f32[1,256,256,8]{2,1,0,3:T(8,128)} async-done(((f32[1,256,256,8]{2,1,0,3:T(8,128)}), f32[1,256,256,8]{2,1,0,3:T(8,128)}, u32[]{:S(2)}, u32[]{:S(2)}) %all-to-all-start.1) | async-done | bytes 2097184 | tf_op jit(solution)/shard_map/all_to_all | solution.py:85
  102.7 3.6 all-to-all-start
  107.8 9.4 %fusion.80 = f32[1,256,256,8]{1,2,3,0:T(8,128)} fusion(f32[]{:T(128)} %bitcast.201, f32[256]{0:T(256)S(1)} %fusion.189, f32[256,8]{0,1:T(8,128)S(1)} %multiply_multiply_fusion, f32[]{:T(128)} %bitcast.2), kind=kLoop, calls=%fused_computation.92 | loop fusion | flops 3670016 | bytes 2106376 | tf_op jit(solution)/shard_map/mul | solution.py:93
  117.2 6.0 %fusion.28 = f32[256,256,8]{1,2,0:T(8,128)} fusion(f32[1,256,256,8]{2,1,0,3:T(8,128)} %all-to-all-done.1), kind=kOutput, calls=%fused_computation.37 | convolution fusion | flops 50332608 | bytes 4194304 | tf_op jit(solution)/shard_map/uhqb,bn->uhqn/dot_general | solution.py:25
  123.2 6.1 %fusion.26 = f32[256,256,8]{1,2,0:T(8,128)} fusion(f32[1,256,256,8]{2,1,0,3:T(8,128)} %all-to-all-done.1), kind=kOutput, calls=%fused_computation.35 | convolution fusion | flops 50332544 | bytes 4194304 | tf_op jit(solution)/shard_map/uhqb,bn->uhqn/dot_general | solution.py:30
  129.2 25.6 %all-to-all-done = f32[1,256,256,8]{2,1,0,3:T(8,128)S(1)} async-done(((f32[1,256,256,8]{2,1,0,3:T(8,128)}), f32[1,256,256,8]{2,1,0,3:T(8,128)S(1)}, u32[]{:S(2)}, u32[]{:S(2)}) %all-to-all-start) | async-done | bytes 2097184 | tf_op jit(solution)/shard_map/all_to_all | solution.py:84
  154.8 5.1 %fusion.68 = f32[256,256,8]{1,2,0:T(8,128)S(1)} fusion(f32[256,256,8]{1,2,0:T(8,128)} %fusion.28, f32[1,256,256,8]{2,1,0,3:T(8,128)S(1)} %all-to-all-done), kind=kOutput, calls=%fused_computation.86 | convolution fusion | flops 50856832 | bytes 6291456 | tf_op jit(solution)/shard_map/uhqb,bn->uhqn/dot_general | solution.py:25
  159.9 3.8 multiply_subtract_fusion.1
  170.3 13.1 %bitcast_multiply_fusion.1 = f32[1,256,256,8]{1,2,3,0:T(8,128)} fusion(f32[256,256,8]{1,0,2:T(8,128)S(1)} %fusion.40, f32[256,256,8]{1,2,0:T(8,128)S(1)} %get-tuple-element.12, f32[]{:T(128)} %bitcast.200, f32[256]{0:T(256)S(1)} %fusion.189, f32[256,8]{0,1:T(8,128)S(1)} %multiply_multiply_fusion, f32[]{:T(128)} %bitcast.2), kind=kOutput, calls=%fused_computation.10 | convolution fusion | flops 1615724544 | bytes 6300680 | tf_op jit(solution)/shard_map/pcrk,rj->pcjk/dot_general | solution.py:25
  183.4 12.9 %bitcast_multiply_fusion = f32[1,256,256,8]{1,2,3,0:T(8,128)} fusion(f32[256,256,8]{1,0,2:T(8,128)S(1)} %fusion.38, f32[256,256,8]{1,2,0:T(8,128)S(1)} %get-tuple-element.12, f32[]{:T(128)} %bitcast.202, f32[256]{0:T(256)S(1)} %fusion.189, f32[256,8]{0,1:T(8,128)S(1)} %multiply_multiply_fusion, f32[]{:T(128)} %bitcast.2), kind=kOutput, calls=%fused_computation.9 | convolution fusion | flops 1615790080 | bytes 6300680 | tf_op jit(solution)/shard_map/pcrk,rj->pcjk/dot_general | solution.py:28
  196.4 118.8 %all-reduce.3.cloned.1.call-done = (f32[1,256,256,8]{1,2,3,0:T(8,128)}, f32[1,256,256,8]{1,2,3,0:T(8,128)}, f32[1,256,256,8]{1,2,3,0:T(8,128)}) async-done(((f32[1,256,256,8]{1,2,3,0:T(8,128)}, f32[1,256,256,8]{1,2,3,0:T(8,128)}, f32[1,256,256,8]{1,2,3,0:T(8,128)}), (f32[1,256,256,8]{1,2,3,0:T(8,128)}, f32[1,256,256,8]{1,2,3,0:T(8,128)}, f32[1,256,256,8]{1,2,3,0:T(8,128)})) %all-reduce.3.cloned.1.call-update) | async-done | bytes 6291472 | tf_op jit(solution)/shard_map/psum | solution.py:94
  315.2 5.4 %fusion.18 = f32[256,256,8]{1,0,2:T(8,128)S(1)} fusion(f32[1,256,256,8]{1,2,3,0:T(8,128)} %get-tuple-element.5, f32[1,256,256,8]{1,2,3,0:T(8,128)} %get-tuple-element.6), kind=kOutput, calls=%fused_computation.27 | convolution fusion | flops 1613103104 | bytes 6291456 | tf_op jit(solution)/shard_map/pcjk,rj->pcrk/dot_general | solution.py:30
  320.7 3.3 fusion.20
  327.2 5.7 %fusion.17 = (f32[256,256,8]{0,1,2:T(8,128)}, f32[256,256,8]{0,1,2:T(8,128)}) fusion(f32[256,256,8]{1,0,2:T(8,128)S(1)} %fusion.74, f32[256,8]{0,1:T(8,128)S(1)} %fusion.160, f32[256,8]{0,1:T(8,128)S(1)} %get-tuple-element.18, f32[256,256,8]{1,0,2:T(8,128)S(1)} %fusion.18, f32[1,256,256,8]{1,2,3,0:T(8,128)S(1)} %copy-done.8, ...), kind=kOutput, calls=%fused_computation.24 | convolution fusion | flops 1616773120 | bytes 12599296 | tf_op jit(solution)/shard_map/pcjk,rj->pcrk/dot_general | solution.py:28
  340.9 3.6 multiply_bitcast_fusion.1
  346.5 5.5 %all-to-all-start.2 = ((f32[1,256,256,8]{2,1,0,3:T(8,128)}), f32[1,256,256,8]{2,1,0,3:T(8,128)}, u32[]{:S(2)}, u32[]{:S(2)}) async-start(f32[1,256,256,8]{2,1,0,3:T(8,128)} %copy.113), calls=%async_computation.2 | async-start | bytes 4194304 | tf_op jit(solution)/shard_map/all_to_all | solution.py:112
  352.0 3.5 fusion.142
  359.6 40.4 %all-to-all-done.2 = f32[1,256,256,8]{2,1,0,3:T(8,128)} async-done(((f32[1,256,256,8]{2,1,0,3:T(8,128)}), f32[1,256,256,8]{2,1,0,3:T(8,128)}, u32[]{:S(2)}, u32[]{:S(2)}) %all-to-all-start.2) | async-done | bytes 2097184 | tf_op jit(solution)/shard_map/all_to_all | solution.py:112
  400.0 3.8 all-to-all-start.3
  403.8 6.1 %fusion.10 = f32[256,256,8]{1,2,0:T(8,128)} fusion(f32[1,256,256,8]{2,1,0,3:T(8,128)} %all-to-all-done.2), kind=kOutput, calls=%fused_computation.15 | convolution fusion | flops 50332544 | bytes 4194304 | tf_op jit(solution)/shard_map/pcrq,nq->pcrn/dot_general | solution.py:28
  409.9 5.9 %fusion.12 = f32[256,256,8]{1,2,0:T(8,128)} fusion(f32[1,256,256,8]{2,1,0,3:T(8,128)} %all-to-all-done.2), kind=kOutput, calls=%fused_computation.17 | convolution fusion | flops 50332544 | bytes 4194304 | tf_op jit(solution)/shard_map/pcrq,nq->pcrn/dot_general | solution.py:25
  415.8 36.3 %all-to-all-done.3 = f32[1,256,256,8]{2,1,0,3:T(8,128)S(1)} async-done(((f32[1,256,256,8]{2,1,0,3:T(8,128)}), f32[1,256,256,8]{2,1,0,3:T(8,128)S(1)}, u32[]{:S(2)}, u32[]{:S(2)}) %all-to-all-start.3) | async-done | bytes 2097184 | tf_op jit(solution)/shard_map/all_to_all | solution.py:113
  455.1 3.3 fusion.8
  477.7 5.3 %copy.125 = f32[2,256,2048]{2,1,0:T(8,128)} copy(f32[2,256,2048]{1,2,0:T(8,128)} %maximum_multiply_fusion) | data formatting | bytes 8388608 | tf_op jit(solution)/shard_map/div | solution.py:129
  (53 shorter events, 65.4 us)
Async XLA Ops:
  27.8 5.4 %copy-start = (f32[256,256,8]{1,0,2:T(8,128)}, f32[256,256,8]{1,0,2:T(8,128)S(1)}, u32[]{:S(2)}) copy-start(f32[256,256,8]{1,0,2:T(8,128)S(1)} %copy.80) | copy-start | bytes 6291460
  27.8 5.4 %copy-start.4 = (f32[256,256,8]{1,0,2:T(8,128)S(1)}, f32[256,256,8]{1,0,2:T(8,128)}, u32[]{:S(2)}) copy-start(f32[256,256,8]{1,0,2:T(8,128)} %fusion.90) | copy-start | bytes 6291460
  38.4 3.2 copy-start.1
  47.1 55.6 %all-to-all-start.1 = ((f32[1,256,256,8]{2,1,0,3:T(8,128)}), f32[1,256,256,8]{2,1,0,3:T(8,128)}, u32[]{:S(2)}, u32[]{:S(2)}) async-start(f32[1,256,256,8]{2,1,0,3:T(8,128)} %copy.94), calls=%async_computation.1 | async-start | bytes 4194304 | tf_op jit(solution)/shard_map/all_to_all | solution.py:85
  102.7 52.1 %all-to-all-start = ((f32[1,256,256,8]{2,1,0,3:T(8,128)}), f32[1,256,256,8]{2,1,0,3:T(8,128)S(1)}, u32[]{:S(2)}, u32[]{:S(2)}) async-start(f32[1,256,256,8]{2,1,0,3:T(8,128)} %copy.87), calls=%async_computation | async-start | bytes 4194304 | tf_op jit(solution)/shard_map/all_to_all | solution.py:84
  106.4 208.8 %all-reduce.3.cloned.1.call-start = ((), (), s32[]{:S(2)}) async-start(), calls=%async_computation.4 | async-start | bytes 12582912 | tf_op jit(solution)/shard_map/psum | solution.py:94
  154.8 5.1 %copy-start.3 = (f32[256,256,8]{1,2,0:T(8,128)S(1)}, f32[256,256,8]{1,2,0:T(8,128)}, u32[]{:S(2)}) copy-start(f32[256,256,8]{1,2,0:T(8,128)} %fusion.26) | copy-start | bytes 6291460
  315.2 5.5 %copy-start.7 = (f32[1,256,256,8]{1,2,3,0:T(8,128)S(1)}, f32[1,256,256,8]{1,2,3,0:T(8,128)}, u32[]{:S(2)}) copy-start(f32[1,256,256,8]{1,2,3,0:T(8,128)} %get-tuple-element.6) | copy-start | bytes 6291460
  315.2 5.5 %copy-start.9 = (f32[1,256,256,8]{1,2,3,0:T(8,128)S(1)}, f32[1,256,256,8]{1,2,3,0:T(8,128)}, u32[]{:S(2)}) copy-start(f32[1,256,256,8]{1,2,3,0:T(8,128)} %get-tuple-element.5) | copy-start | bytes 6291460
  320.7 3.3 copy-start.8
  335.1 3.2 copy-start.2
  346.5 53.5 %all-to-all-start.2 = ((f32[1,256,256,8]{2,1,0,3:T(8,128)}), f32[1,256,256,8]{2,1,0,3:T(8,128)}, u32[]{:S(2)}, u32[]{:S(2)}) async-start(f32[1,256,256,8]{2,1,0,3:T(8,128)} %copy.113), calls=%async_computation.2 | async-start | bytes 4194304 | tf_op jit(solution)/shard_map/all_to_all | solution.py:112
  400.0 52.1 %all-to-all-start.3 = ((f32[1,256,256,8]{2,1,0,3:T(8,128)}), f32[1,256,256,8]{2,1,0,3:T(8,128)S(1)}, u32[]{:S(2)}, u32[]{:S(2)}) async-start(f32[1,256,256,8]{2,1,0,3:T(8,128)} %copy.117), calls=%async_computation.3 | async-start | bytes 4194304 | tf_op jit(solution)/shard_map/all_to_all | solution.py:113
  455.1 3.3 copy-start.5
  455.1 3.3 copy-start.6
Sparse Core Ops, SparseCore 0:
  196.4 118.6 all-reduce.2
where the time goes:
time: 497 us; the launch traced here: 490 us
  waiting for transfers between devices  260 us (52%)
  matrix products  147 us (30%)
  local copies, waits for them, and re-layouts  33.6 us (7%)
  starting transfers between devices  20.2 us (4%)
  between operations  15.5 us (3%)
  other arithmetic  14.5 us (3%)
    psum x1, waiting for transfers between devices, body(): totals = lax.psum((summands[0], summands[1], summands[2]), 'dist')  119 us
    all_to_all x1, waiting for transfers between devices, body(): lax.all_to_all(backward_real, 'pix', split_axis=3, concat_axis=3, tiled=T...  40.4 us
    dot_general x7, matrix products, complex_product(): jnp.einsum(pattern, real_part, sine_part, precision=lax.Precision.HIGHEST)  39.8 us
    all_to_all x1, waiting for transfers between devices, body(): lax.all_to_all(spec_imag, 'pix', split_axis=3, concat_axis=3, tiled=True)  38.4 us
    dot_general x7, matrix products, complex_product(): jnp.einsum(pattern, real_part, cosine, precision=lax.Precision.HIGHEST)  37.9 us
    all_to_all x1, waiting for transfers between devices, body(): lax.all_to_all(backward_imaginary, 'pix', split_axis=3, concat_axis=3, ti...  36.3 us
    dot_general x7, matrix products, complex_product(): jnp.einsum(pattern, imag_part, sine_part, precision=lax.Precision.HIGHEST)  29.5 us
    dot_general x7, matrix products, complex_product(): jnp.einsum(pattern, imag_part, cosine, precision=lax.Precision.HIGHEST)  28.2 us
  transfers between devices with their start and end apart: 5, of which 5 were waited for; matrix products, arithmetic and copies ran while one was open for 10% of the time, Pallas kernels for 0%

commit v1 on v0

--- a/solution.py
+++ b/solution.py
@@ -6,6 +6,17 @@
 
 ABSORB_RATIO = 0.1
 REGULARIZER = 0.05
+
+
+def cut_along(value, dim, length):
+    before, after = (value.shape[:dim], value.shape[dim + 1 :])
+    return jnp.moveaxis(value.reshape(*before, length, -1, *after), dim, 0)
+
+
+def laid_out(blocks, dim):
+    blocks = jnp.moveaxis(blocks, 0, dim)
+    shape = blocks.shape
+    return blocks.reshape(*shape[:dim], shape[dim] * shape[dim + 1], *shape[dim + 2 :])
 
 
 def unit_phase(first_len, second_len, period):
@@ -81,7 +92,15 @@
         + signed_square(col_freq, columns)[:, None, None]
     )
     own_gain = transfer(defocus[0], blurring[0], squared)
-    received_real = lax.all_to_all(spec_real, "pix", split_axis=3, concat_axis=3, tiled=True)
+    peers, index = (lax.axis_size("pix"), lax.axis_index("pix"))
+    parts = cut_along(spec_real, 3, peers)
+    out = parts
+    for lap in range(1, peers):
+        target, source = ((index + lap) % peers, (index - lap) % peers)
+        sent = lax.dynamic_index_in_dim(parts, target, 0)
+        other = lax.ppermute(sent, "pix", [(i, (i + lap) % peers) for i in range(peers)])
+        out = lax.dynamic_update_slice_in_dim(out, other, source, axis=0)
+    received_real = laid_out(out, 3)
     received_imaginary = lax.all_to_all(spec_imag, "pix", split_axis=3, concat_axis=3, tiled=True)
     middle_real, middle_imaginary = complex_product(
         "uhqb,bn->uhqn", received_real, received_imaginary, pixel_lookup_table

time: 497 us -> 520 us (1.046)
  local copies, waits for them, and re-layouts: 33.6 us -> 61.3 us
  starting transfers between devices: 20.2 us -> 31.5 us
  matrix products: 147 us -> 137 us
  waiting for transfers between devices: 260 us -> 253 us
    all_to_all x1, waiting for transfers between devices: 38.4 us -> 0.01 us  [body(): lax.all_to_all(spec_imag, 'pix', split_axis=3, concat_axis=3, tiled=True)]
    ppermute x0 -> x7, waiting for transfers between devices: none -> 37.2 us  [body(): lax.ppermute(sent, 'pix', [(i, (i + lap) % peers) for i in range(peers)])]
    dynamic_update_slice x0 -> x7, local copies, waits for them, and re-layouts: none -> 27.4 us  [body(): out = lax.dynamic_update_slice_in_dim(out, other, source, axis=0)]
    all_to_all x1 -> x0, waiting for transfers between devices: 25.6 us -> none  [body(): lax.all_to_all(spec_real, 'pix', split_axis=3, concat_axis=3, tiled=True)]
    psum x1, waiting for transfers between devices: 119 us -> 139 us  [body(): totals = lax.psum((summands[0], summands[1], summands[2]), 'dist')]
    ppermute x0 -> x7, starting transfers between devices: none -> 14.7 us  [body(): lax.ppermute(sent, 'pix', [(i, (i + lap) % peers) for i in range(peers)])]
  transfers between devices with their start and end apart: 5 -> 11, of which waited for: 5 -> 5; matrix products, arithmetic and copies ran while one was open for 10% -> 13% of each run, Pallas kernels for 0% -> 0%
where the time goes in v1:
time: 520 us; the launch traced here: 513 us
  waiting for transfers between devices  253 us (49%)
  matrix products  137 us (26%)
  local copies, waits for them, and re-layouts  61.3 us (12%)
  starting transfers between devices  31.5 us (6%)
  between operations  15.9 us (3%)
  other arithmetic  14.3 us (3%)
    psum x1, waiting for transfers between devices, body(): totals = lax.psum((summands[0], summands[1], summands[2]), 'dist')  139 us
    all_to_all x1, waiting for transfers between devices, body(): lax.all_to_all(backward_real, 'pix', split_axis=3, concat_axis=3, tiled=T...  40.4 us
    dot_general x7, matrix products, complex_product(): jnp.einsum(pattern, real_part, sine_part, precision=lax.Precision.HIGHEST)  38.6 us
    ppermute x7, waiting for transfers between devices, body(): lax.ppermute(sent, 'pix', [(i, (i + lap) % peers) for i in range(peers)])  37.2 us
    all_to_all x1, waiting for transfers between devices, body(): lax.all_to_all(backward_imaginary, 'pix', split_axis=3, concat_axis=3, ti...  36.2 us
    dot_general x7, matrix products, complex_product(): jnp.einsum(pattern, real_part, cosine, precision=lax.Precision.HIGHEST)  35.1 us
    dynamic_update_slice x7, local copies, waits for them, and re-layouts, body(): out = lax.dynamic_update_slice_in_dim(out, other, source, axis=0)  27.4 us
    dot_general x7, matrix products, complex_product(): jnp.einsum(pattern, imag_part, sine_part, precision=lax.Precision.HIGHEST)  26 us
  transfers between devices with their start and end apart: 11, of which 5 were waited for; matrix products, arithmetic and copies ran while one was open for 13% of the time, Pallas kernels for 0%

profile of v1, /device:TPU:0, one launch (start us, length us, event | category | flops | bytes accessed | tf_op | source)
XLA Modules:
  0.0 512.6 jit_solution(8094186534501393537)
XLA Ops:
  6.6 3.9 fusion.321
  14.3 4.2 fusion.101
  18.5 4.2 fusion.89
  27.9 4.7 convolution_subtract_fusion
  32.6 3.6 multiply_subtract_fusion.2
  39.4 3.6 add_bitcast_fusion.1
  45.0 7.4 %all-to-all-start = ((f32[1,256,256,8]{2,1,0,3:T(8,128)}), f32[1,256,256,8]{2,1,0,3:T(8,128)}, u32[]{:S(2)}, u32[]{:S(2)}) async-start(f32[1,256,256,8]{2,1,0,3:T(8,128)} %copy.92), calls=%async_computation | async-start | bytes 4194304 | tf_op jit(solution)/shard_map/all_to_all | solution.py:104
  72.3 26.1 %collective-permute-done = f32[1,1,256,256,1]{3,0,2,4,1:T(1,128)S(1)} collective-permute-done((f32[1,1,256,256,1]{3,0,2,4,1:T(1,128)}, f32[1,1,256,256,1]{3,0,2,4,1:T(1,128)S(1)}, u32[]{:S(2)}, u32[]{:S(2)}) %collective-permute-start) | collective-permute-done | bytes 262176 | tf_op jit(solution)/shard_map/ppermute | solution.py:101
  98.4 5.2 %collective-permute-start.6 = (f32[1,1,256,256,1]{3,0,2,4,1:T(1,128)}, f32[1,1,256,256,1]{3,0,2,4,1:T(1,128)}, u32[]{:S(2)}, u32[]{:S(2)}) collective-permute-start(f32[1,1,256,256,1]{3,0,2,4,1:T(1,128)} %get-tuple-element.18), channel_id=1, source_target_pairs={{0,7},{1,0},{2,1},{3,2},{4,3},{5,4},{6,5},{7,6},{8,15},{9,8},{10,9... | collective-permute-start | bytes 786440 | tf_op jit(solution)/shard_map/ppermute | solution.py:101
  103.6 9.3 %fusion.79 = f32[1,256,256,8]{1,2,3,0:T(8,128)} fusion(f32[]{:T(128)} %bitcast.218, f32[256]{0:T(256)S(1)} %fusion.220, f32[256,8]{0,1:T(8,128)S(1)} %multiply_multiply_fusion, f32[]{:T(128)} %bitcast.2), kind=kLoop, calls=%fused_computation.90 | loop fusion | flops 3670016 | bytes 2106376 | tf_op jit(solution)/shard_map/mul | solution.py:112
  116.3 3.4 dynamic_update_slice.22
  119.7 11.1 %collective-permute-done.2 = f32[1,1,256,256,1]{3,0,2,4,1:T(1,128)S(1)} collective-permute-done((f32[1,1,256,256,1]{3,0,2,4,1:T(1,128)}, f32[1,1,256,256,1]{3,0,2,4,1:T(1,128)S(1)}, u32[]{:S(2)}, u32[]{:S(2)}) %collective-permute-start.2) | collective-permute-done | bytes 262176 | tf_op jit(solution)/shard_map/ppermute | solution.py:101
  134.2 3.4 dynamic_update_slice.24
  141.1 5.1 dynamic_update_slice.26
  146.2 5.3 %dynamic_update_slice.27 = f32[8,1,256,256,1]{3,0,2,4,1:T(8,128)S(1)} dynamic-update-slice(f32[8,1,256,256,1]{3,0,2,4,1:T(8,128)S(1)} %dynamic_update_slice.26, f32[1,1,256,256,1]{3,0,2,4,1:T(1,128)} %collective-permute-done.6, s32[]{:T(128)S(6)} %select_n.265, s32[]{:T(128)} %constant.165.clone.1, s32[]{:T(128)} %constant.165.clone.1, s32[]{:T(128)} %constant.165.clone.1, s32[]{:T(128)} %constant.165.clone.1) | dynamic-update-slice | bytes 524292 | tf_op jit(solution)/shard_map/dynamic_update_slice | solution.py:102
  151.4 4.7 fusion.32
  158.1 4.7 fusion.30
  165.4 3.5 fusion.40
  172.1 13.1 %bitcast_multiply_fusion.1 = f32[1,256,256,8]{1,2,3,0:T(8,128)} fusion(f32[256,256,8]{1,0,2:T(8,128)S(1)} %fusion.40, f32[256,256,8]{1,2,0:T(8,128)S(1)} %get-tuple-element.12, f32[]{:T(128)} %bitcast.217, f32[256]{0:T(256)S(1)} %fusion.220, f32[256,8]{0,1:T(8,128)S(1)} %multiply_multiply_fusion, f32[]{:T(128)} %bitcast.2), kind=kOutput, calls=%fused_computation.10 | convolution fusion | flops 1615724544 | bytes 6300680 | tf_op jit(solution)/shard_map/pcrk,rj->pcjk/dot_general | solution.py:36
  185.2 12.9 %bitcast_multiply_fusion = f32[1,256,256,8]{1,2,3,0:T(8,128)} fusion(f32[256,256,8]{1,0,2:T(8,128)S(1)} %fusion.38, f32[256,256,8]{1,2,0:T(8,128)S(1)} %get-tuple-element.12, f32[]{:T(128)} %bitcast.219, f32[256]{0:T(256)S(1)} %fusion.220, f32[256,8]{0,1:T(8,128)S(1)} %multiply_multiply_fusion, f32[]{:T(128)} %bitcast.2), kind=kOutput, calls=%fused_computation.9 | convolution fusion | flops 1615790080 | bytes 6300680 | tf_op jit(solution)/shard_map/pcrk,rj->pcjk/dot_general | solution.py:39
  198.2 139.2 %all-reduce.3.cloned.1.call-done = (f32[1,256,256,8]{1,2,3,0:T(8,128)}, f32[1,256,256,8]{1,2,3,0:T(8,128)}, f32[1,256,256,8]{1,2,3,0:T(8,128)}) async-done(((f32[1,256,256,8]{1,2,3,0:T(8,128)}, f32[1,256,256,8]{1,2,3,0:T(8,128)}, f32[1,256,256,8]{1,2,3,0:T(8,128)}), (f32[1,256,256,8]{1,2,3,0:T(8,128)}, f32[1,256,256,8]{1,2,3,0:T(8,128)}, f32[1,256,256,8]{1,2,3,0:T(8,128)})) %all-reduce.3.cloned.1.call-update) | async-done | bytes 6291472 | tf_op jit(solution)/shard_map/psum | solution.py:113
  337.4 5.4 %fusion.18 = f32[256,256,8]{1,0,2:T(8,128)S(1)} fusion(f32[1,256,256,8]{1,2,3,0:T(8,128)} %get-tuple-element.5, f32[1,256,256,8]{1,2,3,0:T(8,128)} %get-tuple-element.6), kind=kOutput, calls=%fused_computation.27 | convolution fusion | flops 1613103104 | bytes 6291456 | tf_op jit(solution)/shard_map/pcjk,rj->pcrk/dot_general | solution.py:41
  349.4 5.7 %fusion.17 = (f32[256,256,8]{0,1,2:T(8,128)}, f32[256,256,8]{0,1,2:T(8,128)}) fusion(f32[256,256,8]{1,0,2:T(8,128)S(1)} %fusion.73, f32[256,8]{0,1:T(8,128)S(1)} %fusion.159, f32[256,8]{0,1:T(8,128)S(1)} %get-tuple-element.25, f32[256,256,8]{1,0,2:T(8,128)S(1)} %fusion.18, f32[1,256,256,8]{1,2,3,0:T(8,128)S(1)} %copy-done.9, ...), kind=kOutput, calls=%fused_computation.24 | convolution fusion | flops 1616773120 | bytes 12599296 | tf_op jit(solution)/shard_map/pcjk,rj->pcrk/dot_general | solution.py:39
  363.2 3.6 multiply_bitcast_fusion.1
  368.8 5.5 %all-to-all-start.1 = ((f32[1,256,256,8]{2,1,0,3:T(8,128)}), f32[1,256,256,8]{2,1,0,3:T(8,128)}, u32[]{:S(2)}, u32[]{:S(2)}) async-start(f32[1,256,256,8]{2,1,0,3:T(8,128)} %copy.111), calls=%async_computation.1 | async-start | bytes 4194304 | tf_op jit(solution)/shard_map/all_to_all | solution.py:131
  374.3 3.5 fusion.141
  381.9 40.4 %all-to-all-done.1 = f32[1,256,256,8]{2,1,0,3:T(8,128)} async-done(((f32[1,256,256,8]{2,1,0,3:T(8,128)}), f32[1,256,256,8]{2,1,0,3:T(8,128)}, u32[]{:S(2)}, u32[]{:S(2)}) %all-to-all-start.1) | async-done | bytes 2097184 | tf_op jit(solution)/shard_map/all_to_all | solution.py:131
  422.3 3.8 all-to-all-start.2
  426.1 6.1 %fusion.10 = f32[256,256,8]{1,2,0:T(8,128)} fusion(f32[1,256,256,8]{2,1,0,3:T(8,128)} %all-to-all-done.1), kind=kOutput, calls=%fused_computation.15 | convolution fusion | flops 50332544 | bytes 4194304 | tf_op jit(solution)/shard_map/pcrq,nq->pcrn/dot_general | solution.py:39
  432.2 5.9 %fusion.12 = f32[256,256,8]{1,2,0:T(8,128)} fusion(f32[1,256,256,8]{2,1,0,3:T(8,128)} %all-to-all-done.1), kind=kOutput, calls=%fused_computation.17 | convolution fusion | flops 50332544 | bytes 4194304 | tf_op jit(solution)/shard_map/pcrq,nq->pcrn/dot_general | solution.py:36
  438.1 36.2 %all-to-all-done.2 = f32[1,256,256,8]{2,1,0,3:T(8,128)S(1)} async-done(((f32[1,256,256,8]{2,1,0,3:T(8,128)}), f32[1,256,256,8]{2,1,0,3:T(8,128)S(1)}, u32[]{:S(2)}, u32[]{:S(2)}) %all-to-all-start.2) | async-done | bytes 2097184 | tf_op jit(solution)/shard_map/all_to_all | solution.py:132
  500.0 5.3 %copy.123 = f32[2,256,2048]{2,1,0:T(8,128)} copy(f32[2,256,2048]{1,2,0:T(8,128)} %maximum_multiply_fusion) | data formatting | bytes 8388608 | tf_op jit(solution)/shard_map/div | solution.py:148
  (74 shorter events, 96.5 us)
Async XLA Ops:
  27.9 4.7 copy-start.5
  36.2 3.2 copy-start.2
  36.2 3.2 copy-start
  45.0 7.6 %copy-start.3 = (f32[256,256,8]{1,0,2:T(8,128)S(1)}, f32[256,256,8]{1,0,2:T(8,128)}, u32[]{:S(2)}) copy-start(f32[256,256,8]{1,0,2:T(8,128)} %copy-done.2) | copy-start | bytes 6291460
  45.0 106.4 %all-to-all-start = ((f32[1,256,256,8]{2,1,0,3:T(8,128)}), f32[1,256,256,8]{2,1,0,3:T(8,128)}, u32[]{:S(2)}, u32[]{:S(2)}) async-start(f32[1,256,256,8]{2,1,0,3:T(8,128)} %copy.92), calls=%async_computation | async-start | bytes 4194304 | tf_op jit(solution)/shard_map/all_to_all | solution.py:104
  52.5 284.9 %all-reduce.3.cloned.1.call-start = ((), (), s32[]{:S(2)}) async-start(), calls=%async_computation.3 | async-start | bytes 12582912 | tf_op jit(solution)/shard_map/psum | solution.py:113
  52.6 3.1 copy-start.1
  61.3 37.1 %collective-permute-start = (f32[1,1,256,256,1]{3,0,2,4,1:T(1,128)}, f32[1,1,256,256,1]{3,0,2,4,1:T(1,128)S(1)}, u32[]{:S(2)}, u32[]{:S(2)}) collective-permute-start(f32[1,1,256,256,1]{3,0,2,4,1:T(1,128)} %get-tuple-element.24), channel_id=1, source_target_pairs={{0,1},{1,2},{2,3},{3,4},{4,5},{5,6},{6,7},{7,0},{8,9},{9,10},{10,1... | collective-permute-start | bytes 786440 | tf_op jit(solution)/shard_map/ppermute | solution.py:101
  63.1 35.3 %collective-permute-start.1 = (f32[1,1,256,256,1]{3,0,2,4,1:T(1,128)}, f32[1,1,256,256,1]{3,0,2,4,1:T(1,128)S(1)}, u32[]{:S(2)}, u32[]{:S(2)}) collective-permute-start(f32[1,1,256,256,1]{3,0,2,4,1:T(1,128)} %get-tuple-element.23), channel_id=1, source_target_pairs={{0,2},{1,3},{2,4},{3,5},{4,6},{5,7},{6,0},{7,1},{8,10},{9,11},{10,... | collective-permute-start | bytes 786440 | tf_op jit(solution)/shard_map/ppermute | solution.py:101
  64.6 66.2 %collective-permute-start.2 = (f32[1,1,256,256,1]{3,0,2,4,1:T(1,128)}, f32[1,1,256,256,1]{3,0,2,4,1:T(1,128)S(1)}, u32[]{:S(2)}, u32[]{:S(2)}) collective-permute-start(f32[1,1,256,256,1]{3,0,2,4,1:T(1,128)} %get-tuple-element.22), channel_id=1, source_target_pairs={{0,3},{1,4},{2,5},{3,6},{4,7},{5,0},{6,1},{7,2},{8,11},{9,12},{10,... | collective-permute-start | bytes 786440 | tf_op jit(solution)/shard_map/ppermute | solution.py:101
  67.0 67.2 %collective-permute-start.3 = (f32[1,1,256,256,1]{3,0,2,4,1:T(1,128)}, f32[1,1,256,256,1]{3,0,2,4,1:T(1,128)S(1)}, u32[]{:S(2)}, u32[]{:S(2)}) collective-permute-start(f32[1,1,256,256,1]{3,0,2,4,1:T(1,128)} %get-tuple-element.21), channel_id=1, source_target_pairs={{0,4},{1,5},{2,6},{3,7},{4,0},{5,1},{6,2},{7,3},{8,12},{9,13},{10,... | collective-permute-start | bytes 786440 | tf_op jit(solution)/shard_map/ppermute | solution.py:101
  68.4 69.2 %collective-permute-start.4 = (f32[1,1,256,256,1]{3,0,2,4,1:T(1,128)}, f32[1,1,256,256,1]{3,0,2,4,1:T(1,128)S(1)}, u32[]{:S(2)}, u32[]{:S(2)}) collective-permute-start(f32[1,1,256,256,1]{3,0,2,4,1:T(1,128)} %get-tuple-element.20), channel_id=1, source_target_pairs={{0,5},{1,6},{2,7},{3,0},{4,1},{5,2},{6,3},{7,4},{8,13},{9,14},{10,... | collective-permute-start | bytes 786440 | tf_op jit(solution)/shard_map/ppermute | solution.py:101
  98.4 42.7 %collective-permute-start.5 = (f32[1,1,256,256,1]{3,0,2,4,1:T(1,128)}, f32[1,1,256,256,1]{3,0,2,4,1:T(1,128)}, u32[]{:S(2)}, u32[]{:S(2)}) collective-permute-start(f32[1,1,256,256,1]{3,0,2,4,1:T(1,128)} %get-tuple-element.19), channel_id=1, source_target_pairs={{0,6},{1,7},{2,0},{3,1},{4,2},{5,3},{6,4},{7,5},{8,14},{9,15},{10,... | collective-permute-start | bytes 786440 | tf_op jit(solution)/shard_map/ppermute | solution.py:101
  98.4 47.8 %collective-permute-start.6 = (f32[1,1,256,256,1]{3,0,2,4,1:T(1,128)}, f32[1,1,256,256,1]{3,0,2,4,1:T(1,128)}, u32[]{:S(2)}, u32[]{:S(2)}) collective-permute-start(f32[1,1,256,256,1]{3,0,2,4,1:T(1,128)} %get-tuple-element.18), channel_id=1, source_target_pairs={{0,7},{1,0},{2,1},{3,2},{4,3},{5,4},{6,5},{7,6},{8,15},{9,8},{10,9... | collective-permute-start | bytes 786440 | tf_op jit(solution)/shard_map/ppermute | solution.py:101
  337.4 5.5 %copy-start.8 = (f32[1,256,256,8]{1,2,3,0:T(8,128)S(1)}, f32[1,256,256,8]{1,2,3,0:T(8,128)}, u32[]{:S(2)}) copy-start(f32[1,256,256,8]{1,2,3,0:T(8,128)} %get-tuple-element.6) | copy-start | bytes 6291460
  337.4 5.5 %copy-start.10 = (f32[1,256,256,8]{1,2,3,0:T(8,128)S(1)}, f32[1,256,256,8]{1,2,3,0:T(8,128)}, u32[]{:S(2)}) copy-start(f32[1,256,256,8]{1,2,3,0:T(8,128)} %get-tuple-element.5) | copy-start | bytes 6291460
  342.9 3.1 copy-start.9
  357.3 3.2 copy-start.4
  368.8 53.5 %all-to-all-start.1 = ((f32[1,256,256,8]{2,1,0,3:T(8,128)}), f32[1,256,256,8]{2,1,0,3:T(8,128)}, u32[]{:S(2)}, u32[]{:S(2)}) async-start(f32[1,256,256,8]{2,1,0,3:T(8,128)} %copy.111), calls=%async_computation.1 | async-start | bytes 4194304 | tf_op jit(solution)/shard_map/all_to_all | solution.py:131
  422.3 52.1 %all-to-all-start.2 = ((f32[1,256,256,8]{2,1,0,3:T(8,128)}), f32[1,256,256,8]{2,1,0,3:T(8,128)S(1)}, u32[]{:S(2)}, u32[]{:S(2)}) async-start(f32[1,256,256,8]{2,1,0,3:T(8,128)} %copy.115), calls=%async_computation.2 | async-start | bytes 4194304 | tf_op jit(solution)/shard_map/all_to_all | solution.py:132
  477.4 3.3 copy-start.6
  477.4 3.3 copy-start.7
Sparse Core Ops, SparseCore 0:
  198.2 139.0 all-reduce.2
